TPU v7x, 32 devices: a whole 2x2x4 slice. The times are simulated.
32 devices in a mesh: orb: 16 (over z, y, core), grid: 2 (over x).
Axes of the slice: x: 2, y: 2, z: 4, core: 2. Of those that a mesh axis runs over, the one named last changes fastest.
Arguments:
- orbitals: bfloat16 [32, 11520], P('orb', 'grid'), may hold values from -1.5 to 1.5
- occupation: bfloat16 [32], P('orb'), may hold values from 0.29882812 to 1
Outputs:
- potentials: float32 [32, 11520], P('orb', 'grid')
- projectors: float32 [32, 11520], P('orb', 'grid')
All inputs are finite; a program needn't handle non-finite values.
Results may differ from a plain program's by a relative error of at most 0.0025.
Values may be sent and summed in bfloat16 or wider, within the bound.
No kernel may reach another device: no remote copies, remote signals or barrier semaphores. Data moves between devices by JAX's collectives and lax.ppermute only.
A program may use at most 64 MiB of HBM per device.

v0:
```python
import math
import jax
import jax.numpy as jnp
from jax import lax
from jax.sharding import PartitionSpec as P

NX = 20
NY = 24
NZ = 24
NPTS = 11520


def hartley_table(length):
    index = jnp.arange(length, dtype=jnp.int32)
    product = index[:, None] * index[None, :] % length
    angle = 2.0 * math.pi / length * product.astype(jnp.float32)
    return (jnp.cos(angle) + jnp.sin(angle)).astype(jnp.bfloat16)


def signed_square(length):
    index = jnp.arange(length, dtype=jnp.int32)
    signed = jnp.where(index <= length // 2, index, index - length).astype(jnp.float32)
    return (2.0 * math.pi * signed / length) ** 2


def coulomb_kernel(size_x, size_y, size_z):
    total = (
        signed_square(size_x)[:, None, None]
        + signed_square(size_y)[None, :, None]
        + signed_square(size_z)[None, None, :]
    )
    safe = jnp.where(total > 0, total, 1.0)
    return jnp.where(total > 0, 1.0 / safe, 0.0) / (size_x * size_y * size_z)


def solve_pairs(density, table_x, table_y, table_z, kernel):
    section = jnp.einsum(
        "ax,pxyz->payz", table_x, density, preferred_element_type=jnp.float32
    ).astype(jnp.bfloat16)
    section = jnp.einsum(
        "by,pxyz->pxbz", table_y, section, preferred_element_type=jnp.float32
    ).astype(jnp.bfloat16)
    spectrum = jnp.einsum("cz,pxyz->pxyc", table_z, section, preferred_element_type=jnp.float32)
    section = (spectrum * kernel).astype(jnp.bfloat16)
    section = jnp.einsum(
        "cz,pxyz->pxyc", table_z, section, preferred_element_type=jnp.float32
    ).astype(jnp.bfloat16)
    section = jnp.einsum(
        "by,pxyz->pxbz", table_y, section, preferred_element_type=jnp.float32
    ).astype(jnp.bfloat16)
    return jnp.einsum("ax,pxyz->payz", table_x, section, preferred_element_type=jnp.float32)


def pair_folder(targets, running, pieces):
    table_x = hartley_table(NX)
    table_y = hartley_table(NY)
    table_z = hartley_table(NZ)
    kernel = coulomb_kernel(NX, NY, NZ)
    target_rows = targets.astype(jnp.float32)
    target_count = targets.shape[0]
    block, block_weight = pieces
    rows = block.shape[0]
    group = math.gcd(rows, 64)
    blocks = block.reshape(rows // group, group, NPTS)
    weights = block_weight.astype(jnp.float32).reshape(rows // group, group)

    def accumulate(totals, inputs):
        sources, source_weight = inputs
        source_rows = sources.astype(jnp.float32)
        density = (target_rows[:, None, :] * source_rows[None, :, :]).astype(jnp.bfloat16)
        density = density.reshape(target_count * group, NX, NY, NZ)
        potential = solve_pairs(density, table_x, table_y, table_z, kernel).reshape(
            target_count, group, NPTS
        )
        weighted = source_weight[None, :, None] * potential * source_rows[None, :, :]
        return (totals - jnp.sum(weighted, axis=1), None)

    result, unused = lax.scan(accumulate, running, (blocks, weights))
    return result


def on_device(orbitals, occupation):
    own_count = orbitals.shape[0]
    per_device = own_count // lax.axis_size("grid")
    empty = jnp.zeros((per_device, NPTS), jnp.float32)
    whole = lax.all_gather(orbitals, "grid", axis=1, tiled=True)
    targets = lax.dynamic_slice_in_dim(whole, lax.axis_index("grid") * per_device, per_device, 0)
    totals = pair_folder(
        targets,
        empty,
        (
            lax.all_gather(whole, "orb", axis=0, tiled=True),
            lax.all_gather(occupation, "orb", axis=0, tiled=True),
        ),
    )
    potentials = lax.all_to_all(totals, "grid", split_axis=1, concat_axis=0, tiled=True)
    source_points, potential_points = (
        lax.all_to_all(
            orbitals.astype(jnp.float32), "orb", split_axis=1, concat_axis=0, tiled=True
        ),
        lax.all_to_all(potentials, "orb", split_axis=1, concat_axis=0, tiled=True),
    )
    partial_gram = (
        lax.dot_general(
            source_points,
            potential_points,
            (((1,), (1,)), ((), ())),
            precision=lax.Precision.HIGHEST,
        )
        / NPTS
    )
    gram = lax.psum(partial_gram, ("orb", "grid"))
    factor = jnp.linalg.cholesky(-gram)
    identity = jnp.eye(gram.shape[0], dtype=jnp.float32)
    inverse = lax.linalg.triangular_solve(factor, identity, left_side=True, lower=True)
    projector_points = jnp.dot(inverse, potential_points, precision=lax.Precision.HIGHEST)
    projectors = lax.all_to_all(projector_points, "orb", split_axis=0, concat_axis=1, tiled=True)
    return (potentials, projectors)


def solution(mesh):
    placed = (P("orb", "grid"), P("orb"))
    return jax.shard_map(
        on_device,
        mesh=mesh,
        in_specs=placed,
        out_specs=(P("orb", "grid"), P("orb", "grid")),
        check_vma=False,
    )
```

profile of v0, /device:TPU:0, one launch (start us, length us, event | category | flops | bytes accessed | tf_op | source)
XLA Modules:
  0.0 226.1 jit_solution(919936937522886090)
XLA Ops:
  0.7 5.7 %all_gather.10 = bf16[2,11520]{1,0:T(2,128)(2,1)S(1)} all-gather(bf16[2,5760]{1,0:T(2,128)(2,1)} %param.2), channel_id=1, replica_groups=mesh['orb'=16,'grid'=2] {'grid'}, dimensions={1}, use_global_device_ids=true | all-gather | bytes 69120 | tf_op jit(solution)/shard_map/all_gather | solution.py:86
  6.3 24.3 %all-gather = bf16[16,2,11520]{2,1,0:T(2,128)(2,1)S(1)} all-gather(bf16[1,2,11520]{2,1,0:T(2,128)(2,1)S(1)} %bitcast.58), channel_id=1, replica_groups=mesh['orb'=16,'grid'=2] {'orb'}, dimensions={0}, use_global_device_ids=true | all-gather | bytes 783360 | tf_op jit(solution)/shard_map/all_gather | solution.py:92
  30.7 6.4 %reshape.167 = f32[32,20,24,24]{3,2,1,0:T(8,128)} reshape(bf16[16,2,11520]{2,1,0:T(2,128)(2,1)S(1)} %all-gather) | data formatting | bytes 2211840 | tf_op jit(solution)/shard_map/while/body/eval_jaxpr/convert_element_type | solution.py:69
  37.1 1.3 reshape.174
  38.8 3.9 %multiply_convert_fusion.1 = bf16[32,20,24,24]{3,2,1,0:T(8,128)(2,1)S(1)} fusion(f32[32,20,24,24]{3,2,1,0:T(8,128)} %reshape.167, f32[20,24,24]{2,1,0:T(8,128)S(1)} %reshape.166), kind=kLoop, calls=%fused_computation.1 | loop fusion | flops 737280 | bytes 2257920 | tf_op jit(solution)/shard_map/while/body/eval_jaxpr/convert_element_type | solution.py:70
  42.6 4.9 %convert_bitcast_fusion = bf16[32,20,24,24]{1,3,2,0:T(8,128)(2,1)} fusion(bf16[32,20,24,24]{3,2,1,0:T(8,128)(2,1)S(1)} %multiply_convert_fusion.1), kind=kOutput, calls=%fused_computation.4 | convolution fusion | flops 15118640 | bytes 1474560 | tf_op jit(solution)/shard_map/while/body/eval_jaxpr/ax,pxyz->payz/dot_general | solution.py:37
  47.5 8.5 %copy.24 = bf16[32,20,24,24]{2,3,1,0:T(8,128)(2,1)} copy(bf16[32,20,24,24]{1,3,2,0:T(8,128)(2,1)} %convert_bitcast_fusion) | data formatting | bytes 1474560 | tf_op jit(solution)/shard_map/while/body/eval_jaxpr/convert_element_type | solution.py:39
  56.0 5.2 %fusion.44 = bf16[32,20,24,24]{3,2,1,0:T(8,128)(2,1)} fusion(bf16[32,20,24,24]{2,3,1,0:T(8,128)(2,1)} %copy.24), kind=kOutput, calls=%fused_computation.53 | convolution fusion | flops 17701056 | bytes 1474560 | tf_op jit(solution)/shard_map/while/body/eval_jaxpr/by,pxyz->pxbz/dot_general | solution.py:40
  61.5 7.4 %fusion.2 = bf16[32,20,24,24]{3,2,1,0:T(8,128)(2,1)} fusion(f32[20,24,24]{2,1,0:T(8,128)S(1)} %fusion.19, bf16[32,20,24,24]{3,2,1,0:T(8,128)(2,1)} %fusion.44), kind=kOutput, calls=%fused_computation.5 | convolution fusion | flops 36139392 | bytes 1520640 | tf_op jit(solution)/shard_map/while/body/eval_jaxpr/cz,pxyz->pxyc/dot_general | solution.py:45
  68.9 5.4 %convert_bitcast_fusion.1 = bf16[32,20,24,24]{2,3,1,0:T(8,128)(2,1)} fusion(bf16[32,20,24,24]{3,2,1,0:T(8,128)(2,1)} %fusion.2), kind=kOutput, calls=%fused_computation.8 | convolution fusion | flops 18069696 | bytes 1474560 | tf_op jit(solution)/shard_map/while/body/eval_jaxpr/by,pxyz->pxbz/dot_general | solution.py:48
  74.3 10.1 %copy.27 = bf16[32,20,24,24]{0,1,3,2:T(8,128)(2,1)S(1)} copy(bf16[32,20,24,24]{2,3,1,0:T(8,128)(2,1)} %convert_bitcast_fusion.1) | data formatting | bytes 1474560 | tf_op jit(solution)/shard_map/while/body/eval_jaxpr/convert_element_type | solution.py:50
  84.4 4.0 %convolution_bitcast_fusion = f32[32,20,24,24]{0,1,3,2:T(8,128)} fusion(bf16[32,20,24,24]{0,1,3,2:T(8,128)(2,1)S(1)} %copy.27), kind=kOutput, calls=%fused_computation.13 | convolution fusion | flops 14750000 | bytes 2211840 | tf_op jit(solution)/shard_map/while/body/eval_jaxpr/ax,pxyz->payz/dot_general | solution.py:51
  88.4 12.1 %copy.28 = f32[32,20,24,24]{3,2,1,0:T(8,128)} copy(f32[32,20,24,24]{0,1,3,2:T(8,128)} %convolution_bitcast_fusion) | data formatting | bytes 2949120 | tf_op jit(solution)/shard_map/while/body/eval_jaxpr/ax,pxyz->payz/transpose | solution.py:51
  102.0 6.8 %reshape.165 = f32[32,11520]{1,0:T(8,128)S(1)} reshape(f32[32,20,24,24]{3,2,1,0:T(8,128)} %copy.28) | data formatting | bytes 2949120 | tf_op jit(solution)/shard_map/while/body/eval_jaxpr/reshape | solution.py:72
  108.9 29.9 %all-reduce = bf16[32]{0:T(256)(128)(2,1)S(1)} all-reduce(bf16[32]{0:T(256)(128)(2,1)S(1)} %dynamic-update-slice.3), channel_id=1, replica_groups=mesh['orb'=16,'grid'=2] {'orb'}, use_global_device_ids=true, to_apply=%add | all-reduce | flops 32 | bytes 128
  139.1 0.7 sub.25
  139.7 3.3 %all-to-all-start = ((f32[1,2,5760]{2,0,1:T(1,128)}), f32[1,2,5760]{2,0,1:T(1,128)S(1)}, u32[]{:S(2)}, u32[]{:S(2)}) async-start(f32[1,2,5760]{2,0,1:T(1,128)} %sub.25), calls=%async_computation | async-start | bytes 92160 | tf_op jit(solution)/shard_map/all_to_all | solution.py:96
  143.8 3.2 %all-to-all-done = f32[1,2,5760]{2,0,1:T(1,128)S(1)} async-done(((f32[1,2,5760]{2,0,1:T(1,128)}), f32[1,2,5760]{2,0,1:T(1,128)S(1)}, u32[]{:S(2)}, u32[]{:S(2)}) %all-to-all-start) | async-done | bytes 46112 | tf_op jit(solution)/shard_map/all_to_all | solution.py:96
  147.0 3.5 %all-to-all-start.2 = ((f32[2,16,360]{2,0,1:T(2,128)}), f32[2,16,360]{2,0,1:T(2,128)S(1)}, u32[]{:S(2)}, u32[]{:S(2)}) async-start(f32[2,16,360]{2,0,1:T(2,128)} %copy.30), calls=%async_computation.2 | async-start | bytes 98304 | tf_op jit(solution)/shard_map/all_to_all | solution.py:98
  150.8 0.6 copy.29
  151.4 5.8 %all-to-all-done.2 = f32[2,16,360]{2,0,1:T(2,128)S(1)} async-done(((f32[2,16,360]{2,0,1:T(2,128)}), f32[2,16,360]{2,0,1:T(2,128)S(1)}, u32[]{:S(2)}, u32[]{:S(2)}) %all-to-all-start.2) | async-done | bytes 46112 | tf_op jit(solution)/shard_map/all_to_all | solution.py:98
  157.3 3.5 %all-to-all-start.1 = ((f32[2,16,360]{2,0,1:T(2,128)}), f32[2,16,360]{2,0,1:T(2,128)S(1)}, u32[]{:S(2)}, u32[]{:S(2)}) async-start(f32[2,16,360]{2,0,1:T(2,128)} %copy.29), calls=%async_computation.1 | async-start | bytes 98304 | tf_op jit(solution)/shard_map/all_to_all | solution.py:101
  160.8 6.7 %all-to-all-done.1 = f32[2,16,360]{2,0,1:T(2,128)S(1)} async-done(((f32[2,16,360]{2,0,1:T(2,128)}), f32[2,16,360]{2,0,1:T(2,128)S(1)}, u32[]{:S(2)}, u32[]{:S(2)}) %all-to-all-start.1) | async-done | bytes 46112 | tf_op jit(solution)/shard_map/all_to_all | solution.py:101
  167.8 38.0 %psum.7 = f32[32,32]{0,1:T(8,128)S(1)} all-reduce(f32[32,32]{0,1:T(8,128)S(1)} %fusion.17), channel_id=1, replica_groups=mesh['orb'=16,'grid'=2] {'orb','grid'}, use_global_device_ids=true, to_apply=%region_1.2 | all-reduce | flops 1024 | bytes 8192 | tf_op jit(solution)/shard_map/psum | solution.py:112
  205.8 2.9 %cholesky.17 = f32[32,32]{1,0:T(8,128)S(1)} custom-call(f32[32,32]{1,0:T(8,128)S(1)} %fusion.22), custom_call_target="Cholesky" | custom-call | tf_op jit(solution)/shard_map/jit(cholesky)/cholesky | solution.py:113
  208.8 0.6 compare_reduce_fusion
  209.4 0.7 fusion.21
  210.1 2.4 %custom-call.6 = f32[1,32,32]{1,2,0:T(8,128)S(1)} custom-call(f32[1,32,32]{2,1,0:T(8,128)S(1)} %fusion.21), custom_call_target="InvertDiagBlocksLowerTriangular" | custom-call | tf_op jit(solution)/shard_map/triangular_solve | solution.py:115
  213.0 0.6 copy.34
  213.6 5.0 %all-to-all-start.3 = ((f32[16,2,360]{2,1,0:T(2,128)}), f32[16,2,360]{2,1,0:T(2,128)S(1)}, u32[]{:S(2)}, u32[]{:S(2)}) async-start(f32[16,2,360]{2,1,0:T(2,128)} %copy.34), calls=%async_computation.3 | async-start | bytes 98304 | tf_op jit(solution)/shard_map/all_to_all | solution.py:117
  219.3 6.1 %all-to-all-done.3 = f32[16,2,360]{2,1,0:T(2,128)S(1)} async-done(((f32[16,2,360]{2,1,0:T(2,128)}), f32[16,2,360]{2,1,0:T(2,128)S(1)}, u32[]{:S(2)}, u32[]{:S(2)}) %all-to-all-start.3) | async-done | bytes 46112 | tf_op jit(solution)/shard_map/all_to_all | solution.py:117
  225.4 0.8 all_to_all.65
  (37 shorter events, 4.2 us)
Async XLA Ops:
  88.4 12.1 %copy-start.3 = (u32[32]{0:T(128)S(1)}, u32[32]{0:T(128)}, u32[]{:S(2)}) copy-start(u32[32]{0:T(128)} %constant.125) | copy-start | bytes 388
  88.4 13.4 %copy-start.2 = (bf16[2]{0:T(256)(128)(2,1)S(1)}, bf16[2]{0:T(256)(128)(2,1)}, u32[]{:S(2)}) copy-start(bf16[2]{0:T(256)(128)(2,1)} %param.3) | copy-start | bytes 16
  102.0 36.7 %copy-start = (f32[32,11520]{1,0:T(8,128)S(1)}, f32[32,11520]{1,0:T(8,128)}, u32[]{:S(2)}) copy-start(f32[32,11520]{1,0:T(8,128)} %reshape.174) | copy-start | bytes 4423684
  102.0 41.0 %copy-start.1 = (bf16[2,5760]{1,0:T(2,128)(2,1)S(1)}, bf16[2,5760]{1,0:T(2,128)(2,1)}, u32[]{:S(2)}) copy-start(bf16[2,5760]{1,0:T(2,128)(2,1)} %param.2) | copy-start | bytes 69124
  139.7 7.3 %all-to-all-start = ((f32[1,2,5760]{2,0,1:T(1,128)}), f32[1,2,5760]{2,0,1:T(1,128)S(1)}, u32[]{:S(2)}, u32[]{:S(2)}) async-start(f32[1,2,5760]{2,0,1:T(1,128)} %sub.25), calls=%async_computation | async-start | bytes 92160 | tf_op jit(solution)/shard_map/all_to_all | solution.py:96
  147.0 10.2 %all-to-all-start.2 = ((f32[2,16,360]{2,0,1:T(2,128)}), f32[2,16,360]{2,0,1:T(2,128)S(1)}, u32[]{:S(2)}, u32[]{:S(2)}) async-start(f32[2,16,360]{2,0,1:T(2,128)} %copy.30), calls=%async_computation.2 | async-start | bytes 98304 | tf_op jit(solution)/shard_map/all_to_all | solution.py:98
  157.3 10.2 %all-to-all-start.1 = ((f32[2,16,360]{2,0,1:T(2,128)}), f32[2,16,360]{2,0,1:T(2,128)S(1)}, u32[]{:S(2)}, u32[]{:S(2)}) async-start(f32[2,16,360]{2,0,1:T(2,128)} %copy.29), calls=%async_computation.1 | async-start | bytes 98304 | tf_op jit(solution)/shard_map/all_to_all | solution.py:101
  213.6 11.8 %all-to-all-start.3 = ((f32[16,2,360]{2,1,0:T(2,128)}), f32[16,2,360]{2,1,0:T(2,128)S(1)}, u32[]{:S(2)}, u32[]{:S(2)}) async-start(f32[16,2,360]{2,1,0:T(2,128)} %copy.34), calls=%async_computation.3 | async-start | bytes 98304 | tf_op jit(solution)/shard_map/all_to_all | solution.py:117
where the time goes:
time: 227 us; the launch traced here: 226 us
  blocking collectives  97.9 us (43%)
  local copies, waits for them, and re-layouts  50.8 us (22%)
  matrix products  27.5 us (12%)
  waiting for transfers between devices  21.9 us (10%)
  starting transfers between devices  15.3 us (7%)
  other arithmetic  11.4 us (5%)
    psum x1, blocking collectives, on_device(): gram = lax.psum(partial_gram, ('orb', 'grid'))  38 us
    unnamed x1, blocking collectives  29.9 us
    all_gather x1, blocking collectives, on_device(): lax.all_gather(whole, 'orb', axis=0, tiled=True)  24.3 us
    transpose x1, local copies, waits for them, and re-layouts, solve_pairs(): jnp.einsum('ax,pxyz->payz', table_x, section, preferred_element_type=jnp....  12.1 us
    dot_general x2, matrix products, solve_pairs(): jnp.einsum('by,pxyz->pxbz', table_y, section, preferred_element_type=jnp....  10.6 us
    convert_element_type x1, local copies, waits for them, and re-layouts, solve_pairs(): section = jnp.einsum('by,pxyz->pxbz', table_y, section, preferred_element...  10.1 us
    convert_element_type x1, local copies, waits for them, and re-layouts, solve_pairs(): section = jnp.einsum('ax,pxyz->payz', table_x, density, preferred_element...  8.51 us
    convert_element_type x2, local copies, waits for them, and re-layouts, accumulate(): source_rows = sources.astype(jnp.float32)  7.76 us
  transfers between devices with their start and end apart: 4, of which 4 were waited for; matrix products, arithmetic and copies ran while one was open for 1% of the time, Pallas kernels for 0%

commit v1 on v0

--- a/solution.py
+++ b/solution.py
@@ -80,6 +80,12 @@
 
 
 def on_device(orbitals, occupation):
+
+    def register_set_all(mine):
+        return jnp.concatenate(
+            lax.all_to_all(jnp.stack(jnp.split(mine, lax.axis_size("orb"), 0), 0), "orb", 0, 0), 1
+        )
+
     own_count = orbitals.shape[0]
     per_device = own_count // lax.axis_size("grid")
     empty = jnp.zeros((per_device, NPTS), jnp.float32)
@@ -114,7 +120,7 @@
     identity = jnp.eye(gram.shape[0], dtype=jnp.float32)
     inverse = lax.linalg.triangular_solve(factor, identity, left_side=True, lower=True)
     projector_points = jnp.dot(inverse, potential_points, precision=lax.Precision.HIGHEST)
-    projectors = lax.all_to_all(projector_points, "orb", split_axis=0, concat_axis=1, tiled=True)
+    projectors = register_set_all(projector_points)
     return (potentials, projectors)
 
 

time: 227 us -> 236 us (1.040)
  local copies, waits for them, and re-layouts: 50.8 us -> 59.5 us
    unnamed x12 -> x27, local copies, waits for them, and re-layouts: 1.49 us -> 10.3 us
where the time goes in v1:
time: 236 us; the launch traced here: 235 us
  blocking collectives  97.9 us (41%)
  local copies, waits for them, and re-layouts  59.5 us (25%)
  matrix products  27.6 us (12%)
  waiting for transfers between devices  21.9 us (9%)
  starting transfers between devices  15.3 us (6%)
  other arithmetic  11.4 us (5%)
    psum x1, blocking collectives, on_device(): gram = lax.psum(partial_gram, ('orb', 'grid'))  38 us
    unnamed x1, blocking collectives  29.9 us
    all_gather x1, blocking collectives, on_device(): lax.all_gather(whole, 'orb', axis=0, tiled=True)  24.3 us
    transpose x1, local copies, waits for them, and re-layouts, solve_pairs(): jnp.einsum('ax,pxyz->payz', table_x, section, preferred_element_type=jnp....  12.1 us
    dot_general x2, matrix products, solve_pairs(): jnp.einsum('by,pxyz->pxbz', table_y, section, preferred_element_type=jnp....  10.6 us
    unnamed x27, local copies, waits for them, and re-layouts  10.3 us
    convert_element_type x1, local copies, waits for them, and re-layouts, solve_pairs(): section = jnp.einsum('by,pxyz->pxbz', table_y, section, preferred_element...  10.1 us
    convert_element_type x1, local copies, waits for them, and re-layouts, solve_pairs(): section = jnp.einsum('ax,pxyz->payz', table_x, density, preferred_element...  8.51 us
  transfers between devices with their start and end apart: 4, of which 4 were waited for; matrix products, arithmetic and copies ran while one was open for 1% of the time, Pallas kernels for 0%

profile of v1, /device:TPU:0, one launch (start us, length us, event | category | flops | bytes accessed | tf_op | source)
XLA Modules:
  0.0 234.9 jit_solution(9939405017746769419)
XLA Ops:
  0.7 5.7 %all_gather.10 = bf16[2,11520]{1,0:T(2,128)(2,1)S(1)} all-gather(bf16[2,5760]{1,0:T(2,128)(2,1)} %param.2), channel_id=1, replica_groups=mesh['orb'=16,'grid'=2] {'grid'}, dimensions={1}, use_global_device_ids=true | all-gather | bytes 69120 | tf_op jit(solution)/shard_map/all_gather | solution.py:92
  6.3 24.3 %all-gather = bf16[16,2,11520]{2,1,0:T(2,128)(2,1)S(1)} all-gather(bf16[1,2,11520]{2,1,0:T(2,128)(2,1)S(1)} %bitcast.119), channel_id=1, replica_groups=mesh['orb'=16,'grid'=2] {'orb'}, dimensions={0}, use_global_device_ids=true | all-gather | bytes 783360 | tf_op jit(solution)/shard_map/all_gather | solution.py:98
  30.7 6.4 %reshape.169 = f32[32,20,24,24]{3,2,1,0:T(8,128)} reshape(bf16[16,2,11520]{2,1,0:T(2,128)(2,1)S(1)} %all-gather) | data formatting | bytes 2211840 | tf_op jit(solution)/shard_map/while/body/eval_jaxpr/convert_element_type | solution.py:69
  37.1 1.3 reshape.176
  38.8 3.9 %multiply_convert_fusion.1 = bf16[32,20,24,24]{3,2,1,0:T(8,128)(2,1)S(1)} fusion(f32[32,20,24,24]{3,2,1,0:T(8,128)} %reshape.169, f32[20,24,24]{2,1,0:T(8,128)S(1)} %reshape.168), kind=kLoop, calls=%fused_computation.1 | loop fusion | flops 737280 | bytes 2257920 | tf_op jit(solution)/shard_map/while/body/eval_jaxpr/convert_element_type | solution.py:70
  42.6 4.9 %convert_bitcast_fusion = bf16[32,20,24,24]{1,3,2,0:T(8,128)(2,1)} fusion(bf16[32,20,24,24]{3,2,1,0:T(8,128)(2,1)S(1)} %multiply_convert_fusion.1), kind=kOutput, calls=%fused_computation.4 | convolution fusion | flops 15118640 | bytes 1474560 | tf_op jit(solution)/shard_map/while/body/eval_jaxpr/ax,pxyz->payz/dot_general | solution.py:37
  47.5 8.5 %copy.11 = bf16[32,20,24,24]{2,3,1,0:T(8,128)(2,1)} copy(bf16[32,20,24,24]{1,3,2,0:T(8,128)(2,1)} %convert_bitcast_fusion) | data formatting | bytes 1474560 | tf_op jit(solution)/shard_map/while/body/eval_jaxpr/convert_element_type | solution.py:39
  56.0 5.2 %fusion.42 = bf16[32,20,24,24]{3,2,1,0:T(8,128)(2,1)} fusion(bf16[32,20,24,24]{2,3,1,0:T(8,128)(2,1)} %copy.11), kind=kOutput, calls=%fused_computation.68 | convolution fusion | flops 17701056 | bytes 1474560 | tf_op jit(solution)/shard_map/while/body/eval_jaxpr/by,pxyz->pxbz/dot_general | solution.py:40
  61.5 7.4 %fusion.2 = bf16[32,20,24,24]{3,2,1,0:T(8,128)(2,1)} fusion(f32[20,24,24]{2,1,0:T(8,128)S(1)} %fusion.19, bf16[32,20,24,24]{3,2,1,0:T(8,128)(2,1)} %fusion.42), kind=kOutput, calls=%fused_computation.5 | convolution fusion | flops 36139392 | bytes 1520640 | tf_op jit(solution)/shard_map/while/body/eval_jaxpr/cz,pxyz->pxyc/dot_general | solution.py:45
  68.9 5.4 %convert_bitcast_fusion.1 = bf16[32,20,24,24]{2,3,1,0:T(8,128)(2,1)} fusion(bf16[32,20,24,24]{3,2,1,0:T(8,128)(2,1)} %fusion.2), kind=kOutput, calls=%fused_computation.8 | convolution fusion | flops 18069696 | bytes 1474560 | tf_op jit(solution)/shard_map/while/body/eval_jaxpr/by,pxyz->pxbz/dot_general | solution.py:48
  74.3 10.1 %copy.14 = bf16[32,20,24,24]{0,1,3,2:T(8,128)(2,1)S(1)} copy(bf16[32,20,24,24]{2,3,1,0:T(8,128)(2,1)} %convert_bitcast_fusion.1) | data formatting | bytes 1474560 | tf_op jit(solution)/shard_map/while/body/eval_jaxpr/convert_element_type | solution.py:50
  84.4 4.0 %convolution_bitcast_fusion = f32[32,20,24,24]{0,1,3,2:T(8,128)} fusion(bf16[32,20,24,24]{0,1,3,2:T(8,128)(2,1)S(1)} %copy.14), kind=kOutput, calls=%fused_computation.13 | convolution fusion | flops 14750000 | bytes 2211840 | tf_op jit(solution)/shard_map/while/body/eval_jaxpr/ax,pxyz->payz/dot_general | solution.py:51
  88.4 12.1 %copy.15 = f32[32,20,24,24]{3,2,1,0:T(8,128)} copy(f32[32,20,24,24]{0,1,3,2:T(8,128)} %convolution_bitcast_fusion) | data formatting | bytes 2949120 | tf_op jit(solution)/shard_map/while/body/eval_jaxpr/ax,pxyz->payz/transpose | solution.py:51
  102.0 6.8 %reshape.165 = f32[32,11520]{1,0:T(8,128)S(1)} reshape(f32[32,20,24,24]{3,2,1,0:T(8,128)} %copy.15) | data formatting | bytes 2949120 | tf_op jit(solution)/shard_map/while/body/eval_jaxpr/reshape | solution.py:72
  108.9 29.9 %all-reduce = bf16[32]{0:T(256)(128)(2,1)S(1)} all-reduce(bf16[32]{0:T(256)(128)(2,1)S(1)} %dynamic-update-slice.3), channel_id=1, replica_groups=mesh['orb'=16,'grid'=2] {'orb'}, use_global_device_ids=true, to_apply=%add | all-reduce | flops 32 | bytes 128
  139.1 0.7 sub.25
  139.7 3.3 %all-to-all-start = ((f32[1,2,5760]{2,0,1:T(1,128)}), f32[1,2,5760]{2,0,1:T(1,128)S(1)}, u32[]{:S(2)}, u32[]{:S(2)}) async-start(f32[1,2,5760]{2,0,1:T(1,128)} %sub.25), calls=%async_computation | async-start | bytes 92160 | tf_op jit(solution)/shard_map/all_to_all | solution.py:102
  143.8 3.2 %all-to-all-done = f32[1,2,5760]{2,0,1:T(1,128)S(1)} async-done(((f32[1,2,5760]{2,0,1:T(1,128)}), f32[1,2,5760]{2,0,1:T(1,128)S(1)}, u32[]{:S(2)}, u32[]{:S(2)}) %all-to-all-start) | async-done | bytes 46112 | tf_op jit(solution)/shard_map/all_to_all | solution.py:102
  147.0 3.5 %all-to-all-start.2 = ((f32[2,16,360]{2,0,1:T(2,128)}), f32[2,16,360]{2,0,1:T(2,128)S(1)}, u32[]{:S(2)}, u32[]{:S(2)}) async-start(f32[2,16,360]{2,0,1:T(2,128)} %copy.17), calls=%async_computation.2 | async-start | bytes 98304 | tf_op jit(solution)/shard_map/all_to_all | solution.py:104
  150.8 0.6 copy.16
  151.4 5.8 %all-to-all-done.2 = f32[2,16,360]{2,0,1:T(2,128)S(1)} async-done(((f32[2,16,360]{2,0,1:T(2,128)}), f32[2,16,360]{2,0,1:T(2,128)S(1)}, u32[]{:S(2)}, u32[]{:S(2)}) %all-to-all-start.2) | async-done | bytes 46112 | tf_op jit(solution)/shard_map/all_to_all | solution.py:104
  157.3 3.5 %all-to-all-start.1 = ((f32[2,16,360]{2,0,1:T(2,128)}), f32[2,16,360]{2,0,1:T(2,128)S(1)}, u32[]{:S(2)}, u32[]{:S(2)}) async-start(f32[2,16,360]{2,0,1:T(2,128)} %copy.16), calls=%async_computation.1 | async-start | bytes 98304 | tf_op jit(solution)/shard_map/all_to_all | solution.py:107
  160.8 6.7 %all-to-all-done.1 = f32[2,16,360]{2,0,1:T(2,128)S(1)} async-done(((f32[2,16,360]{2,0,1:T(2,128)}), f32[2,16,360]{2,0,1:T(2,128)S(1)}, u32[]{:S(2)}, u32[]{:S(2)}) %all-to-all-start.1) | async-done | bytes 46112 | tf_op jit(solution)/shard_map/all_to_all | solution.py:107
  167.7 38.0 %psum.7 = f32[32,32]{0,1:T(8,128)S(1)} all-reduce(f32[32,32]{0,1:T(8,128)S(1)} %fusion.17), channel_id=1, replica_groups=mesh['orb'=16,'grid'=2] {'orb','grid'}, use_global_device_ids=true, to_apply=%region_1.2 | all-reduce | flops 1024 | bytes 8192 | tf_op jit(solution)/shard_map/psum | solution.py:118
  205.8 2.9 %cholesky.17 = f32[32,32]{1,0:T(8,128)S(1)} custom-call(f32[32,32]{1,0:T(8,128)S(1)} %fusion.24), custom_call_target="Cholesky" | custom-call | tf_op jit(solution)/shard_map/jit(cholesky)/cholesky | solution.py:119
  208.8 0.6 compare_reduce_fusion
  209.4 0.7 fusion.21
  210.1 2.4 %custom-call.6 = f32[1,32,32]{1,2,0:T(8,128)S(1)} custom-call(f32[1,32,32]{2,1,0:T(8,128)S(1)} %fusion.21), custom_call_target="InvertDiagBlocksLowerTriangular" | custom-call | tf_op jit(solution)/shard_map/triangular_solve | solution.py:121
  222.4 5.0 %all-to-all-start.3 = ((f32[16,2,360]{2,1,0:T(2,128)}), f32[16,2,360]{2,1,0:T(2,128)S(1)}, u32[]{:S(2)}, u32[]{:S(2)}) async-start(f32[16,2,360]{2,1,0:T(2,128)} %constant_dynamic-update-slice_fusion), calls=%async_computation.3 | async-start | bytes 98304 | tf_op jit(solution)/shard_map/all_to_all | solution.py:86
  227.4 0.6 copy.30
  228.0 6.1 %all-to-all-done.3 = f32[16,2,360]{2,1,0:T(2,128)S(1)} async-done(((f32[16,2,360]{2,1,0:T(2,128)}), f32[16,2,360]{2,1,0:T(2,128)S(1)}, u32[]{:S(2)}, u32[]{:S(2)}) %all-to-all-start.3) | async-done | bytes 46112 | tf_op jit(solution)/shard_map/all_to_all | solution.py:86
  234.1 0.8 reshape.167
  (50 shorter events, 12.9 us)
Async XLA Ops:
  88.4 12.1 %copy-start.3 = (u32[32]{0:T(128)S(1)}, u32[32]{0:T(128)}, u32[]{:S(2)}) copy-start(u32[32]{0:T(128)} %constant.125) | copy-start | bytes 388
  88.4 13.4 %copy-start.2 = (bf16[2]{0:T(256)(128)(2,1)S(1)}, bf16[2]{0:T(256)(128)(2,1)}, u32[]{:S(2)}) copy-start(bf16[2]{0:T(256)(128)(2,1)} %param.3) | copy-start | bytes 16
  102.0 36.7 %copy-start = (f32[32,11520]{1,0:T(8,128)S(1)}, f32[32,11520]{1,0:T(8,128)}, u32[]{:S(2)}) copy-start(f32[32,11520]{1,0:T(8,128)} %reshape.176) | copy-start | bytes 4423684
  102.0 41.0 %copy-start.1 = (bf16[2,5760]{1,0:T(2,128)(2,1)S(1)}, bf16[2,5760]{1,0:T(2,128)(2,1)}, u32[]{:S(2)}) copy-start(bf16[2,5760]{1,0:T(2,128)(2,1)} %param.2) | copy-start | bytes 69124
  139.7 7.3 %all-to-all-start = ((f32[1,2,5760]{2,0,1:T(1,128)}), f32[1,2,5760]{2,0,1:T(1,128)S(1)}, u32[]{:S(2)}, u32[]{:S(2)}) async-start(f32[1,2,5760]{2,0,1:T(1,128)} %sub.25), calls=%async_computation | async-start | bytes 92160 | tf_op jit(solution)/shard_map/all_to_all | solution.py:102
  147.0 10.2 %all-to-all-start.2 = ((f32[2,16,360]{2,0,1:T(2,128)}), f32[2,16,360]{2,0,1:T(2,128)S(1)}, u32[]{:S(2)}, u32[]{:S(2)}) async-start(f32[2,16,360]{2,0,1:T(2,128)} %copy.17), calls=%async_computation.2 | async-start | bytes 98304 | tf_op jit(solution)/shard_map/all_to_all | solution.py:104
  157.3 10.2 %all-to-all-start.1 = ((f32[2,16,360]{2,0,1:T(2,128)}), f32[2,16,360]{2,0,1:T(2,128)S(1)}, u32[]{:S(2)}, u32[]{:S(2)}) async-start(f32[2,16,360]{2,0,1:T(2,128)} %copy.16), calls=%async_computation.1 | async-start | bytes 98304 | tf_op jit(solution)/shard_map/all_to_all | solution.py:107
  222.4 11.8 %all-to-all-start.3 = ((f32[16,2,360]{2,1,0:T(2,128)}), f32[16,2,360]{2,1,0:T(2,128)S(1)}, u32[]{:S(2)}, u32[]{:S(2)}) async-start(f32[16,2,360]{2,1,0:T(2,128)} %constant_dynamic-update-slice_fusion), calls=%async_computation.3 | async-start | bytes 98304 | tf_op jit(solution)/shard_map/all_to_all | solution.py:86
